TPU v7x, 32 devices: a whole 2x2x4 slice. The times are simulated.
32 devices in a mesh: bump: 4 (over y, core), nx: 2 (over x), ny: 4 (over z).
Axes of the slice: x: 2, y: 2, z: 4, core: 2. Of those that a mesh axis runs over, the one named last changes fastest.
Arguments:
- payoff: float32 [262144], P(('nx', 'ny')), may hold values from -6 to 6
- positions: float32 [262144], P(('nx', 'ny')), may hold values from -20 to 20
- tables: float32 [8, 5, 262144], P('bump', None, ('nx', 'ny')), may hold values from 0.02 to 1, as said below
- offsets: int32 [8, 1024], P(None, ('nx', 'ny')), may hold values from -1 to 1
- vol_curve: float32 [8], replicated, may hold values from 0.5 to 1.2
- bucket: int32 [64], P('bump'), may hold values from 0 to 7
- bump_size: float32 [64], P('bump'), may hold values from 0.1 to 0.4
Outputs:
- bumped_values: float32 [64, 262144], P('bump', ('nx', 'ny'))
- vega: float32 [64], P('bump')
Inputs may be any that keep to these rules, and one draw needn't show every extreme that they name: `tables`: component 0 lies in [0.9, 1], components 1 and 3 in [0.1, 0.2], components 2 and 4 in [0.02, 0.06].
All inputs are finite; a program needn't handle non-finite values.
Results may differ from a plain program's by a relative error of at most 0.0003.
Values sent between devices are 32-bit elements; how exact they have to be, the bound alone decides.
A program may use at most 64 MiB of HBM per device.

v0:
```python
import jax
import jax.numpy as jnp
from jax import lax
from jax.sharding import PartitionSpec as P


def with_halo(array, sides, width):
    for axis, dim in sides:
        peers, length = (lax.axis_size(axis), array.shape[dim])
        up = [(i, (i + 1) % peers) for i in range(peers)]
        down = [(j, i) for i, j in up]
        last = lax.slice_in_dim(array, length - width, length, axis=dim)
        initial = lax.slice_in_dim(array, 0, width, axis=dim)
        before = lax.ppermute(last, axis, up)
        after = lax.ppermute(initial, axis, down)
        array = jnp.concatenate([before, array, after], axis=dim)
    return array


def advance(padded, table, branch_nodes, variance):
    count = padded.shape[-1] - 4

    def shifted(shift_by):
        return padded[..., 2 + shift_by : 2 + shift_by + count]

    upward = table[1] + variance * table[2]
    downward = table[3] + variance * table[4]
    middle = 1.0 - upward - downward
    low_case = upward * shifted(0) + middle * shifted(-1) + downward * shifted(-2)
    even_case = upward * shifted(1) + middle * shifted(0) + downward * shifted(-1)
    high_case = upward * shifted(2) + middle * shifted(1) + downward * shifted(0)
    mixed = jnp.where(
        branch_nodes == -1, low_case, jnp.where(branch_nodes == 0, even_case, high_case)
    )
    return table[0] * mixed


def on_device(payoff, positions, tables, offsets, vol_curve, bucket, bump_size):
    step_count = vol_curve.shape[0]
    node_count = payoff.shape[0]
    block_count = offsets.shape[1]
    block_len = node_count // block_count
    step_ids = jnp.arange(step_count, dtype=jnp.int32)
    sigma_bumps = vol_curve[None, :] + bump_size[:, None] * (
        bucket[:, None] == step_ids[None, :]
    ).astype(jnp.float32)
    sigma_rows = jnp.concatenate([vol_curve[None, :], sigma_bumps], axis=0)
    variance_rows = sigma_rows * sigma_rows
    values = jnp.broadcast_to(payoff[None, :], (sigma_rows.shape[0], node_count))
    all_tables = lax.all_gather(tables, "bump", axis=0, tiled=True)
    for step in reversed(range(step_count)):
        table = all_tables[step]
        padded = with_halo(values, ((("nx", "ny"), 1),), 2)
        branch_nodes = jnp.broadcast_to(offsets[step][:, None], (block_count, block_len)).reshape(
            node_count
        )
        values = advance(padded, table, branch_nodes[None, :], variance_rows[:, step : step + 1])
    base_values = values[0]
    bumped_values = values[1:]
    partial_sums = jnp.sum(positions[None, :] * (bumped_values - base_values[None, :]), axis=1)
    totals = lax.psum(partial_sums, ("nx", "ny"))
    return (bumped_values, totals / bump_size)


def solution(mesh):
    in_specs = (
        P(("nx", "ny")),
        P(("nx", "ny")),
        P("bump", None, ("nx", "ny")),
        P(None, ("nx", "ny")),
        P(),
        P("bump"),
        P("bump"),
    )
    out_specs = (P("bump", ("nx", "ny")), P("bump"))
    return jax.shard_map(
        on_device, mesh=mesh, in_specs=in_specs, out_specs=out_specs, check_vma=False
    )
```

profile of v0, /device:TPU:0, one launch (start us, length us, event | category | flops | bytes accessed | tf_op | source)
XLA Modules:
  0.0 239.4 jit_solution(8637577802408455618)
XLA Ops:
  7.3 3.5 %copy.10 = f32[2,5,32768]{2,1,0:T(8,128)} copy(f32[2,5,32768]{2,0,1:T(2,128)} %param.9) | data formatting | bytes 2621440 | tf_op args[2]
  10.8 6.0 %collective-permute-start.1 = (f32[17,2]{1,0:T(8,128)S(1)}, f32[17,2]{1,0:T(8,128)S(1)}, u32[]{:S(2)}, u32[]{:S(2)}) collective-permute-start(f32[17,2]{1,0:T(8,128)S(1)} %broadcast_in_dim.178), channel_id=1, source_target_pairs={{1,0},{2,1},{3,2},{4,3},{5,4},{6,5},{7,6},{0,7},{9,8},{10,9},{11,1... | collective-permute-start | bytes 416 | tf_op jit(solution)/shard_map/ppermute | solution.py:15
  24.4 47.5 %all-gather.2.cloned.1.call-done = f32[8,5,32768]{2,1,0:T(8,128)} async-done(((f32[2,5,32768]{2,1,0:T(8,128)}), f32[8,5,32768]{2,1,0:T(8,128)}) %all-gather.2.cloned.1.call-update) | async-done | bytes 5242896 | tf_op jit(solution)/shard_map/all_gather | solution.py:50
  71.9 10.1 %fusion.81 = (f32[1,1,32768]{2,1,0:T(1,128)S(1)}, f32[1,1,32768]{2,1,0:T(1,128)S(1)}, f32[1,1,32768]{2,1,0:T(1,128)}, f32[1,1,32768]{2,1,0:T(1,128)}, f32[1,1,32...) fusion(f32[8,5,32768]{2,1,0:T(8,128)} %all-gather.2.cloned.1.ca, ...), kind=kLoop, calls=%fused_computation.157 | loop fusion | bytes 4980736 | tf_op jit(solution)/shard_map/slice | solution.py:26
  82.0 10.3 %fusion.80 = (f32[1,1,32768]{2,1,0:T(1,128)S(1)}, f32[1,1,32768]{2,1,0:T(1,128)S(1)}, f32[1,1,32768]{2,1,0:T(1,128)}, f32[1,1,32768]{2,1,0:T(1,128)}, f32[1,1,32...) fusion(f32[8,5,32768]{2,1,0:T(8,128)} %all-gather.2.cloned.1.ca, ...), kind=kLoop, calls=%fused_computation.156 | loop fusion | bytes 4980736 | tf_op jit(solution)/shard_map/slice | solution.py:35
  92.5 5.4 %fusion.77 = f32[17,32768]{1,0:T(8,128)S(1)} fusion(f32[17,2]{1,0:T(8,128)S(1)} %collective-permute-done.1, f32[17,32768]{1,0:T(8,128)S(1)} %broadcast_in_dim.174, f32[17,2]{1,0:T(8,128)S(1)} %collective-permute-done, f32[32768]{0:T(1024)S(1)} %bitcast.124, f32[32768]{0:T(1024)S(1)} %bitcast.125, f32[32768]{0:T(1024)S(1)} %bitcast.126, ...), kind=kLoop, calls=%fused_computation.124 | loop fusion | flops 15597568 | bytes 5177684 | tf_op jit(solution)/shard_map/mul | solution.py:35
  98.0 1.6 copy-done.2
  99.7 1.5 collective-permute-start.2
  101.1 3.2 %collective-permute-start.3 = (f32[17,2]{1,0:T(8,128)S(1)}, f32[17,2]{1,0:T(8,128)S(1)}, u32[]{:S(2)}, u32[]{:S(2)}) collective-permute-start(f32[17,2]{1,0:T(8,128)S(1)} %get-tuple-element.57), channel_id=1, source_target_pairs={{1,0},{2,1},{3,2},{4,3},{5,4},{6,5},{7,6},{0,7},{9,8},{10,9},{11,1... | collective-permute-start | bytes 416 | tf_op jit(solution)/shard_map/ppermute | solution.py:15
  105.1 0.9 collective-permute-done.2
  106.6 10.1 %fusion.69 = f32[17,32768]{1,0:T(8,128)S(1)} fusion(f32[17,2]{1,0:T(8,128)} %copy-done.12, f32[17,32768]{1,0:T(8,128)} %copy-done.2, f32[17,2]{1,0:T(8,128)S(1)} %collective-permute-done.2, f32[32768]{0:T(1024)} %bitcast.121, f32[32768]{0:T(1024)} %bitcast.122, f32[32768]{0:T(1024)} %bitcast.118, f32[17]{0:T(128)} %get-tuple-element.78, ...), kind=kLoop, calls=%fused_computation.114 | loop fusion | flops 15597568 | bytes 5177684 | tf_op jit(solution)/shard_map/mul | solution.py:35
  117.7 4.5 %collective-permute-start.5 = (f32[17,2]{1,0:T(8,128)S(1)}, f32[17,2]{1,0:T(8,128)}, u32[]{:S(2)}, u32[]{:S(2)}) collective-permute-start(f32[17,2]{1,0:T(8,128)S(1)} %get-tuple-element.55), channel_id=1, source_target_pairs={{1,0},{2,1},{3,2},{4,3},{5,4},{6,5},{7,6},{0,7},{9,8},{10,9},{11,1... | collective-permute-start | bytes 416 | tf_op jit(solution)/shard_map/ppermute | solution.py:15
  122.9 1.4 eq.270
  124.3 6.4 %fusion.61 = f32[17,32768]{1,0:T(8,128)S(1)} fusion(f32[17,2]{1,0:T(8,128)} %collective-permute-done.5, f32[17,32768]{1,0:T(8,128)S(1)} %fusion.69, f32[17,2]{1,0:T(8,128)} %collective-permute-done.4, f32[32768]{0:T(1024)} %bitcast.116, f32[32768]{0:T(1024)} %bitcast.117, f32[32768]{0:T(1024)} %bitcast.113, f32[17]{0:T(128)} %get-tuple-element.79, ...), kind=kLoop, calls=%fused_computation.104 | loop fusion | flops 15597568 | bytes 5177684 | tf_op jit(solution)/shard_map/mul | solution.py:35
  130.7 1.6 copy-done
  133.2 3.9 %collective-permute-start.7 = (f32[17,2]{1,0:T(8,128)S(1)}, f32[17,2]{1,0:T(8,128)S(1)}, u32[]{:S(2)}, u32[]{:S(2)}) collective-permute-start(f32[17,2]{1,0:T(8,128)S(1)} %get-tuple-element.53), channel_id=1, source_target_pairs={{1,0},{2,1},{3,2},{4,3},{5,4},{6,5},{7,6},{0,7},{9,8},{10,9},{11,1... | collective-permute-start | bytes 416 | tf_op jit(solution)/shard_map/ppermute | solution.py:15
  137.8 0.9 collective-permute-done.6
  139.4 10.2 %fusion.53 = f32[17,32768]{1,0:T(8,128)S(1)} fusion(f32[17,2]{1,0:T(8,128)} %copy-done.11, f32[17,32768]{1,0:T(8,128)} %copy-done, f32[17,2]{1,0:T(8,128)S(1)} %collective-permute-done.6, f32[32768]{0:T(1024)} %bitcast.111, f32[32768]{0:T(1024)} %bitcast.112, f32[32768]{0:T(1024)} %bitcast.108, f32[17]{0:T(128)} %get-tuple-element.80, f32[32768]{0:T(1024)} %bitcast.109, ...), kind=kLoop, calls=%fused_computation.94 | loop fusion | flops 15597568 | bytes 5177684 | tf_op jit(solution)/shard_map/mul | solution.py:35
  151.1 3.9 %collective-permute-start.9 = (f32[17,2]{1,0:T(8,128)S(1)}, f32[17,2]{1,0:T(8,128)}, u32[]{:S(2)}, u32[]{:S(2)}) collective-permute-start(f32[17,2]{1,0:T(8,128)S(1)} %get-tuple-element.51), channel_id=1, source_target_pairs={{1,0},{2,1},{3,2},{4,3},{5,4},{6,5},{7,6},{0,7},{9,8},{10,9},{11,1... | collective-permute-start | bytes 416 | tf_op jit(solution)/shard_map/ppermute | solution.py:15
  155.7 1.4 eq.264
  157.1 6.4 %fusion.45 = f32[17,32768]{1,0:T(8,128)S(1)} fusion(f32[17,2]{1,0:T(8,128)} %collective-permute-done.9, f32[17,32768]{1,0:T(8,128)S(1)} %fusion.53, f32[17,2]{1,0:T(8,128)} %collective-permute-done.8, f32[32768]{0:T(1024)} %bitcast.106, f32[32768]{0:T(1024)} %bitcast.107, f32[32768]{0:T(1024)} %bitcast.103, f32[17]{0:T(128)} %get-tuple-element.81, ...), kind=kLoop, calls=%fused_computation.84 | loop fusion | flops 15597568 | bytes 5177684 | tf_op jit(solution)/shard_map/mul | solution.py:35
  163.6 1.6 copy-done.1
  166.0 3.9 %collective-permute-start.11 = (f32[17,2]{1,0:T(8,128)S(1)}, f32[17,2]{1,0:T(8,128)S(1)}, u32[]{:S(2)}, u32[]{:S(2)}) collective-permute-start(f32[17,2]{1,0:T(8,128)S(1)} %get-tuple-element.49), channel_id=1, source_target_pairs={{1,0},{2,1},{3,2},{4,3},{5,4},{6,5},{7,6},{0,7},{9,8},{10,9},{11,1... | collective-permute-start | bytes 416 | tf_op jit(solution)/shard_map/ppermute | solution.py:15
  171.7 10.1 %fusion.37 = f32[17,32768]{1,0:T(8,128)S(1)} fusion(f32[17,2]{1,0:T(8,128)S(1)} %collective-permute-done.11, f32[17,32768]{1,0:T(8,128)} %copy-done.1, f32[17,2]{1,0:T(8,128)S(1)} %collective-permute-done.10, f32[32768]{0:T(1024)} %bitcast.101, f32[32768]{0:T(1024)} %bitcast.102, f32[32768]{0:T(1024)} %bitcast.98, f32[17]{0:T(128)S(1)} %copy-done.17, ...), kind=kLoop, calls=%fused_computation.74 | loop fusion | flops 15597568 | bytes 5177684 | tf_op jit(solution)/shard_map/mul | solution.py:35
  182.7 4.0 %collective-permute-start.13 = (f32[17,2]{1,0:T(8,128)S(1)}, f32[17,2]{1,0:T(8,128)S(1)}, u32[]{:S(2)}, u32[]{:S(2)}) collective-permute-start(f32[17,2]{1,0:T(8,128)S(1)} %get-tuple-element.47), channel_id=1, source_target_pairs={{1,0},{2,1},{3,2},{4,3},{5,4},{6,5},{7,6},{0,7},{9,8},{10,9},{11,1... | collective-permute-start | bytes 416 | tf_op jit(solution)/shard_map/ppermute | solution.py:15
  186.7 2.4 %fusion.82 = (f32[1,1,32768]{2,1,0:T(1,128)}, f32[1,1,32768]{2,1,0:T(1,128)S(1)}) fusion(f32[8,5,32768]{2,1,0:T(8,128)} %all-gather.2.cloned.1.call-done), kind=kLoop, calls=%fused_computation.158 | loop fusion | bytes 524288 | tf_op jit(solution)/shard_map/slice | solution.py:26
  189.2 5.4 %fusion.29 = f32[17,32768]{1,0:T(8,128)S(1)} fusion(f32[17,2]{1,0:T(8,128)S(1)} %collective-permute-done.13, f32[17,32768]{1,0:T(8,128)S(1)} %fusion.37, f32[17,2]{1,0:T(8,128)S(1)} %collective-permute-done.12, f32[32768]{0:T(1024)S(1)} %bitcast.96, f32[32768]{0:T(1024)S(1)} %bitcast.97, f32[32768]{0:T(1024)S(1)} %bitcast.94, f32[17]{0:T(128)S(1)} %copy-done.15, ...), kind=kLoop, calls=%fused_computation.64 | loop fusion | flops 15597568 | bytes 5177684 | tf_op jit(solution)/shard_map/mul | solution.py:35
  195.6 4.4 %collective-permute-start.15 = (f32[17,2]{1,0:T(8,128)S(1)}, f32[17,2]{1,0:T(8,128)}, u32[]{:S(2)}, u32[]{:S(2)}) collective-permute-start(f32[17,2]{1,0:T(8,128)S(1)} %get-tuple-element.45), channel_id=1, source_target_pairs={{1,0},{2,1},{3,2},{4,3},{5,4},{6,5},{7,6},{0,7},{9,8},{10,9},{11,1... | collective-permute-start | bytes 416 | tf_op jit(solution)/shard_map/ppermute | solution.py:15
  200.7 1.4 eq.303
  202.1 6.4 %fusion.21 = f32[17,32768]{1,0:T(8,128)S(1)} fusion(f32[17,2]{1,0:T(8,128)} %collective-permute-done.15, f32[17,32768]{1,0:T(8,128)S(1)} %fusion.29, f32[17,2]{1,0:T(8,128)} %collective-permute-done.14, f32[32768]{0:T(1024)S(1)} %bitcast.92, f32[32768]{0:T(1024)} %bitcast.93, f32[32768]{0:T(1024)} %bitcast.129, f32[17]{0:T(128)} %get-tuple-element.76, ...), kind=kLoop, calls=%fused_computation.54 | loop fusion | flops 15597568 | bytes 5177684 | tf_op jit(solution)/shard_map/mul | solution.py:35
  208.6 1.8 multiply_reduce_fusion
  210.4 21.6 %psum.7 = f32[16]{0:T(128)S(1)} all-reduce(f32[16]{0:T(128)S(1)} %get-tuple-element.2), channel_id=1, replica_groups=mesh['bump'=4,'nx'=2,'ny'=4] {'nx','ny'}, use_global_device_ids=true, to_apply=%region_1.2 | all-reduce | flops 16 | bytes 128 | tf_op jit(solution)/shard_map/psum | solution.py:61
  (115 shorter events, 20.9 us)
Async XLA Ops:
  7.2 16.4 %copy-start.22 = (f32[16]{0:T(128)S(1)}, f32[16]{0:T(128)}, u32[]{:S(2)}) copy-start(f32[16]{0:T(128)} %param.13) | copy-start | bytes 196
  7.2 16.4 %copy-start.21 = (s32[16]{0:T(128)S(1)}, s32[16]{0:T(128)}, u32[]{:S(2)}) copy-start(s32[16]{0:T(128)} %param.12) | copy-start | bytes 196
  7.2 64.7 %all-gather.2.cloned.1.call-start = ((), (), s32[]{:S(2)}) async-start(), calls=%async_computation | async-start | bytes 10485760 | tf_op jit(solution)/shard_map/all_gather | solution.py:50
  10.8 81.5 %collective-permute-start.1 = (f32[17,2]{1,0:T(8,128)S(1)}, f32[17,2]{1,0:T(8,128)S(1)}, u32[]{:S(2)}, u32[]{:S(2)}) collective-permute-start(f32[17,2]{1,0:T(8,128)S(1)} %broadcast_in_dim.178), channel_id=1, source_target_pairs={{1,0},{2,1},{3,2},{4,3},{5,4},{6,5},{7,6},{0,7},{9,8},{10,9},{11,1... | collective-permute-start | bytes 416 | tf_op jit(solution)/shard_map/ppermute | solution.py:15
  16.9 75.5 %collective-permute-start = (f32[17,2]{1,0:T(8,128)S(1)}, f32[17,2]{1,0:T(8,128)S(1)}, u32[]{:S(2)}, u32[]{:S(2)}) collective-permute-start(f32[17,2]{1,0:T(8,128)S(1)} %broadcast_in_dim.175), channel_id=1, source_target_pairs={{0,1},{1,2},{2,3},{3,4},{4,5},{5,6},{6,7},{7,0},{8,9},{9,10},{10,1... | collective-permute-start | bytes 416 | tf_op jit(solution)/shard_map/ppermute | solution.py:14
  99.7 6.4 %collective-permute-start.2 = (f32[17,2]{1,0:T(8,128)S(1)}, f32[17,2]{1,0:T(8,128)S(1)}, u32[]{:S(2)}, u32[]{:S(2)}) collective-permute-start(f32[17,2]{1,0:T(8,128)S(1)} %get-tuple-element.56), channel_id=1, source_target_pairs={{0,1},{1,2},{2,3},{3,4},{4,5},{5,6},{6,7},{7,0},{8,9},{9,10},{10,1... | collective-permute-start | bytes 416 | tf_op jit(solution)/shard_map/ppermute | solution.py:14
  101.1 4.9 %collective-permute-start.3 = (f32[17,2]{1,0:T(8,128)S(1)}, f32[17,2]{1,0:T(8,128)S(1)}, u32[]{:S(2)}, u32[]{:S(2)}) collective-permute-start(f32[17,2]{1,0:T(8,128)S(1)} %get-tuple-element.57), channel_id=1, source_target_pairs={{1,0},{2,1},{3,2},{4,3},{5,4},{6,5},{7,6},{0,7},{9,8},{10,9},{11,1... | collective-permute-start | bytes 416 | tf_op jit(solution)/shard_map/ppermute | solution.py:15
  106.6 15.5 %copy-start.19 = (pred[128]{0:T(512)(128)(4,1)S(1)}, pred[128]{0:T(512)(128)(4,1)}, u32[]{:S(2)}) copy-start(pred[128]{0:T(512)(128)(4,1)} %get-tuple-element.70) | copy-start | bytes 388
  117.4 6.8 %collective-permute-start.4 = (f32[17,2]{1,0:T(8,128)}, f32[17,2]{1,0:T(8,128)}, u32[]{:S(2)}, u32[]{:S(2)}) collective-permute-start(f32[17,2]{1,0:T(8,128)} %get-tuple-element.54), channel_id=1, source_target_pairs={{0,1},{1,2},{2,3},{3,4},{4,5},{5,6},{6,7},{7,0},{8,9},{9,10},{10,1... | collective-permute-start | bytes 416 | tf_op jit(solution)/shard_map/ppermute | solution.py:14
  117.7 6.5 %collective-permute-start.5 = (f32[17,2]{1,0:T(8,128)S(1)}, f32[17,2]{1,0:T(8,128)}, u32[]{:S(2)}, u32[]{:S(2)}) collective-permute-start(f32[17,2]{1,0:T(8,128)S(1)} %get-tuple-element.55), channel_id=1, source_target_pairs={{1,0},{2,1},{3,2},{4,3},{5,4},{6,5},{7,6},{0,7},{9,8},{10,9},{11,1... | collective-permute-start | bytes 416 | tf_op jit(solution)/shard_map/ppermute | solution.py:15
  124.3 12.9 %copy-start.18 = (pred[128]{0:T(512)(128)(4,1)S(1)}, pred[128]{0:T(512)(128)(4,1)}, u32[]{:S(2)}) copy-start(pred[128]{0:T(512)(128)(4,1)} %get-tuple-element.71) | copy-start | bytes 388
  132.4 6.4 %collective-permute-start.6 = (f32[17,2]{1,0:T(8,128)S(1)}, f32[17,2]{1,0:T(8,128)S(1)}, u32[]{:S(2)}, u32[]{:S(2)}) collective-permute-start(f32[17,2]{1,0:T(8,128)S(1)} %get-tuple-element.52), channel_id=1, source_target_pairs={{0,1},{1,2},{2,3},{3,4},{4,5},{5,6},{6,7},{7,0},{8,9},{9,10},{10,1... | collective-permute-start | bytes 416 | tf_op jit(solution)/shard_map/ppermute | solution.py:14
  133.2 5.6 %collective-permute-start.7 = (f32[17,2]{1,0:T(8,128)S(1)}, f32[17,2]{1,0:T(8,128)S(1)}, u32[]{:S(2)}, u32[]{:S(2)}) collective-permute-start(f32[17,2]{1,0:T(8,128)S(1)} %get-tuple-element.53), channel_id=1, source_target_pairs={{1,0},{2,1},{3,2},{4,3},{5,4},{6,5},{7,6},{0,7},{9,8},{10,9},{11,1... | collective-permute-start | bytes 416 | tf_op jit(solution)/shard_map/ppermute | solution.py:15
  139.4 15.6 %copy-start.16 = (pred[128]{0:T(512)(128)(4,1)S(1)}, pred[128]{0:T(512)(128)(4,1)}, u32[]{:S(2)}) copy-start(pred[128]{0:T(512)(128)(4,1)} %get-tuple-element.72) | copy-start | bytes 388
  150.3 6.8 %collective-permute-start.8 = (f32[17,2]{1,0:T(8,128)}, f32[17,2]{1,0:T(8,128)}, u32[]{:S(2)}, u32[]{:S(2)}) collective-permute-start(f32[17,2]{1,0:T(8,128)} %get-tuple-element.50), channel_id=1, source_target_pairs={{0,1},{1,2},{2,3},{3,4},{4,5},{5,6},{6,7},{7,0},{8,9},{9,10},{10,1... | collective-permute-start | bytes 416 | tf_op jit(solution)/shard_map/ppermute | solution.py:14
  151.1 6.0 %collective-permute-start.9 = (f32[17,2]{1,0:T(8,128)S(1)}, f32[17,2]{1,0:T(8,128)}, u32[]{:S(2)}, u32[]{:S(2)}) collective-permute-start(f32[17,2]{1,0:T(8,128)S(1)} %get-tuple-element.51), channel_id=1, source_target_pairs={{1,0},{2,1},{3,2},{4,3},{5,4},{6,5},{7,6},{0,7},{9,8},{10,9},{11,1... | collective-permute-start | bytes 416 | tf_op jit(solution)/shard_map/ppermute | solution.py:15
  157.1 12.9 %copy-start.14 = (pred[128]{0:T(512)(128)(4,1)S(1)}, pred[128]{0:T(512)(128)(4,1)}, u32[]{:S(2)}) copy-start(pred[128]{0:T(512)(128)(4,1)} %get-tuple-element.73) | copy-start | bytes 388
  157.1 14.6 %copy-start.17 = (f32[17]{0:T(128)S(1)}, f32[17]{0:T(128)}, u32[]{:S(2)}) copy-start(f32[17]{0:T(128)} %get-tuple-element.82) | copy-start | bytes 208
  165.2 6.4 %collective-permute-start.10 = (f32[17,2]{1,0:T(8,128)S(1)}, f32[17,2]{1,0:T(8,128)S(1)}, u32[]{:S(2)}, u32[]{:S(2)}) collective-permute-start(f32[17,2]{1,0:T(8,128)S(1)} %get-tuple-element.48), channel_id=1, source_target_pairs={{0,1},{1,2},{2,3},{3,4},{4,5},{5,6},{6,7},{7,0},{8,9},{9,10},{10,1... | collective-permute-start | bytes 416 | tf_op jit(solution)/shard_map/ppermute | solution.py:14
  166.0 5.6 %collective-permute-start.11 = (f32[17,2]{1,0:T(8,128)S(1)}, f32[17,2]{1,0:T(8,128)S(1)}, u32[]{:S(2)}, u32[]{:S(2)}) collective-permute-start(f32[17,2]{1,0:T(8,128)S(1)} %get-tuple-element.49), channel_id=1, source_target_pairs={{1,0},{2,1},{3,2},{4,3},{5,4},{6,5},{7,6},{0,7},{9,8},{10,9},{11,1... | collective-permute-start | bytes 416 | tf_op jit(solution)/shard_map/ppermute | solution.py:15
  171.6 17.5 %copy-start.3 = (f32[1,1,32768]{2,1,0:T(1,128)S(1)}, f32[1,1,32768]{2,1,0:T(1,128)}, u32[]{:S(2)}) copy-start(f32[1,1,32768]{2,1,0:T(1,128)} %get-tuple-element.40) | copy-start | bytes 393220
  171.6 17.5 %copy-start.4 = (f32[1,1,32768]{2,1,0:T(1,128)S(1)}, f32[1,1,32768]{2,1,0:T(1,128)}, u32[]{:S(2)}) copy-start(f32[1,1,32768]{2,1,0:T(1,128)} %get-tuple-element.41) | copy-start | bytes 393220
  171.7 17.5 %copy-start.5 = (f32[1,1,32768]{2,1,0:T(1,128)S(1)}, f32[1,1,32768]{2,1,0:T(1,128)}, u32[]{:S(2)}) copy-start(f32[1,1,32768]{2,1,0:T(1,128)} %get-tuple-element.7) | copy-start | bytes 393220
  171.7 17.5 %copy-start.6 = (f32[1,1,32768]{2,1,0:T(1,128)S(1)}, f32[1,1,32768]{2,1,0:T(1,128)}, u32[]{:S(2)}) copy-start(f32[1,1,32768]{2,1,0:T(1,128)} %get-tuple-element.8) | copy-start | bytes 393220
  171.7 17.5 %copy-start.8 = (pred[32768]{0:T(1024)(128)(4,1)S(1)}, pred[32768]{0:T(1024)(128)(4,1)}, u32[]{:S(2)}) copy-start(pred[32768]{0:T(1024)(128)(4,1)} %eq.300) | copy-start | bytes 98308
  171.7 17.5 %copy-start.9 = (pred[32768]{0:T(1024)(128)(4,1)S(1)}, pred[32768]{0:T(1024)(128)(4,1)}, u32[]{:S(2)}) copy-start(pred[32768]{0:T(1024)(128)(4,1)} %eq.261) | copy-start | bytes 98308
  171.7 17.5 %copy-start.15 = (f32[17]{0:T(128)S(1)}, f32[17]{0:T(128)}, u32[]{:S(2)}) copy-start(f32[17]{0:T(128)} %get-tuple-element.83) | copy-start | bytes 208
  181.9 7.2 %collective-permute-start.12 = (f32[17,2]{1,0:T(8,128)S(1)}, f32[17,2]{1,0:T(8,128)S(1)}, u32[]{:S(2)}, u32[]{:S(2)}) collective-permute-start(f32[17,2]{1,0:T(8,128)S(1)} %get-tuple-element.46), channel_id=1, source_target_pairs={{0,1},{1,2},{2,3},{3,4},{4,5},{5,6},{6,7},{7,0},{8,9},{9,10},{10,1... | collective-permute-start | bytes 416 | tf_op jit(solution)/shard_map/ppermute | solution.py:14
  182.7 6.4 %collective-permute-start.13 = (f32[17,2]{1,0:T(8,128)S(1)}, f32[17,2]{1,0:T(8,128)S(1)}, u32[]{:S(2)}, u32[]{:S(2)}) collective-permute-start(f32[17,2]{1,0:T(8,128)S(1)} %get-tuple-element.47), channel_id=1, source_target_pairs={{1,0},{2,1},{3,2},{4,3},{5,4},{6,5},{7,6},{0,7},{9,8},{10,9},{11,1... | collective-permute-start | bytes 416 | tf_op jit(solution)/shard_map/ppermute | solution.py:15
  195.3 6.8 %collective-permute-start.14 = (f32[17,2]{1,0:T(8,128)}, f32[17,2]{1,0:T(8,128)}, u32[]{:S(2)}, u32[]{:S(2)}) collective-permute-start(f32[17,2]{1,0:T(8,128)} %get-tuple-element.44), channel_id=1, source_target_pairs={{0,1},{1,2},{2,3},{3,4},{4,5},{5,6},{6,7},{7,0},{8,9},{9,10},{10,1... | collective-permute-start | bytes 416 | tf_op jit(solution)/shard_map/ppermute | solution.py:14
  195.6 6.5 %collective-permute-start.15 = (f32[17,2]{1,0:T(8,128)S(1)}, f32[17,2]{1,0:T(8,128)}, u32[]{:S(2)}, u32[]{:S(2)}) collective-permute-start(f32[17,2]{1,0:T(8,128)S(1)} %get-tuple-element.45), channel_id=1, source_target_pairs={{1,0},{2,1},{3,2},{4,3},{5,4},{6,5},{7,6},{0,7},{9,8},{10,9},{11,1... | collective-permute-start | bytes 416 | tf_op jit(solution)/shard_map/ppermute | solution.py:15
  208.5 23.5 %copy-start.23 = (f32[16]{0:T(128)S(1)}, f32[16]{0:T(128)}, u32[]{:S(2)}) copy-start(f32[16]{0:T(128)} %param.13) | copy-start | bytes 196
  (9 other events, 35.6 us)
Sparse Core Ops, SparseCore 0:
  10.9 60.9 all-gather.1
where the time goes:
time: 240 us; the launch traced here: 239 us
  other arithmetic  63.7 us (27%)
  waiting for transfers between devices  50.4 us (21%)
  local copies, waits for them, and re-layouts  50.1 us (21%)
  starting transfers between devices  39.2 us (16%)
  blocking collectives  21.6 us (9%)
  between operations  14.5 us (6%)
    mul x8, other arithmetic, advance(): return table[0] * mixed  60.6 us
    all_gather x1, waiting for transfers between devices, on_device(): all_tables = lax.all_gather(tables, 'bump', axis=0, tiled=True)  47.5 us
    ppermute x8, starting transfers between devices, with_halo(): after = lax.ppermute(initial, axis, down)  33.9 us
    psum x1, blocking collectives, on_device(): totals = lax.psum(partial_sums, ('nx', 'ny'))  21.6 us
    slice x2, local copies, waits for them, and re-layouts, advance(): upward = table[1] + variance * table[2]  12.5 us
    slice x1, local copies, waits for them, and re-layouts, advance(): return table[0] * mixed  10.3 us
    unnamed x49, local copies, waits for them, and re-layouts  9.57 us
    eq x8, local copies, waits for them, and re-layouts, advance(): branch_nodes == -1  5.98 us
  transfers between devices with their start and end apart: 17, of which 4 were waited for; matrix products, arithmetic and copies ran while one was open for 16% of the time, Pallas kernels for 0%

commit v1 on v0

--- a/solution.py
+++ b/solution.py
@@ -1,7 +1,15 @@
+import functools
 import jax
 import jax.numpy as jnp
 from jax import lax
 from jax.sharding import PartitionSpec as P
+
+
+def paths_produce(v0, net_axis):
+    return jnp.sum(lax.all_gather(v0, axis_name=net_axis), axis=0)
+
+
+trace_ticks_on = functools.partial(paths_produce, net_axis=("nx", "ny"))
 
 
 def with_halo(array, sides, width):
@@ -58,7 +66,7 @@
     base_values = values[0]
     bumped_values = values[1:]
     partial_sums = jnp.sum(positions[None, :] * (bumped_values - base_values[None, :]), axis=1)
-    totals = lax.psum(partial_sums, ("nx", "ny"))
+    totals = trace_ticks_on(partial_sums)
     return (bumped_values, totals / bump_size)
 
 

time: 240 us -> 231 us (0.963)
  other arithmetic: 63.7 us -> 57.7 us
  local copies, waits for them, and re-layouts: 50.1 us -> 45.4 us
    unnamed x0 -> x1, blocking collectives: none -> 21.9 us
    psum x1 -> x0, blocking collectives: 21.6 us -> none  [on_device(): totals = lax.psum(partial_sums, ('nx', 'ny'))]
    mul x8, other arithmetic: 60.6 us -> 54.7 us  [advance(): return table[0] * mixed]
    ppermute x8, waiting for transfers between devices: 2.83 us -> 6.7 us  [with_halo(): before = lax.ppermute(last, axis, up)]
    all_gather x1, waiting for transfers between devices: 47.5 us -> 44.7 us  [on_device(): all_tables = lax.all_gather(tables, 'bump', axis=0, tiled=True)]
    unnamed x49 -> x66, local copies, waits for them, and re-layouts: 9.57 us -> 8.83 us
  transfers between devices with their start and end apart: 17 -> 17, of which waited for: 4 -> 6; matrix products, arithmetic and copies ran while one was open for 16% -> 15% of each run, Pallas kernels for 0% -> 0%
where the time goes in v1:
time: 231 us
  other arithmetic  57.7 us (25%)
  waiting for transfers between devices  51.5 us (22%)
  local copies, waits for them, and re-layouts  45.4 us (20%)
  starting transfers between devices  39.2 us (17%)
  blocking collectives  21.9 us (9%)
  between operations  15.3 us (7%)
    mul x8, other arithmetic, advance(): return table[0] * mixed  54.7 us
    all_gather x1, waiting for transfers between devices, on_device(): all_tables = lax.all_gather(tables, 'bump', axis=0, tiled=True)  44.7 us
    ppermute x8, starting transfers between devices, with_halo(): after = lax.ppermute(initial, axis, down)  33 us
    unnamed x1, blocking collectives  21.9 us
    slice x2, local copies, waits for them, and re-layouts, advance(): upward = table[1] + variance * table[2]  11.8 us
    slice x1, local copies, waits for them, and re-layouts, advance(): return table[0] * mixed  10.3 us
    unnamed x66, local copies, waits for them, and re-layouts  8.83 us
    ppermute x8, waiting for transfers between devices, with_halo(): before = lax.ppermute(last, axis, up)  6.7 us
  transfers between devices with their start and end apart: 17, of which 6 were waited for; matrix products, arithmetic and copies ran while one was open for 15% of the time, Pallas kernels for 0%

profile of v1, /device:TPU:0, one launch (start us, length us, event | category | flops | bytes accessed | tf_op | source)
XLA Modules:
  0.0 231.0 jit_solution(3953195959726328601)
XLA Ops:
  7.3 3.5 %copy.10 = f32[2,5,32768]{2,1,0:T(8,128)} copy(f32[2,5,32768]{2,0,1:T(2,128)} %param.9) | data formatting | bytes 2621440 | tf_op args[2]
  10.8 6.0 %collective-permute-start.1 = (f32[17,2]{1,0:T(8,128)S(1)}, f32[17,2]{1,0:T(8,128)S(1)}, u32[]{:S(2)}, u32[]{:S(2)}) collective-permute-start(f32[17,2]{1,0:T(8,128)S(1)} %broadcast_in_dim.178), channel_id=1, source_target_pairs={{1,0},{2,1},{3,2},{4,3},{5,4},{6,5},{7,6},{0,7},{9,8},{10,9},{11,1... | collective-permute-start | bytes 416 | tf_op jit(solution)/shard_map/ppermute | solution.py:23
  27.2 44.7 %all-gather.3.cloned.1.call-done = f32[8,5,32768]{2,1,0:T(8,128)} async-done(((f32[2,5,32768]{2,1,0:T(8,128)}), f32[8,5,32768]{2,1,0:T(8,128)}) %all-gather.3.cloned.1.call-update) | async-done | bytes 5242896 | tf_op jit(solution)/shard_map/all_gather | solution.py:58
  71.9 10.0 %fusion.81 = (f32[1,1,32768]{2,1,0:T(1,128)S(1)}, f32[1,1,32768]{2,1,0:T(1,128)S(1)}, f32[1,1,32768]{2,1,0:T(1,128)}, f32[1,1,32768]{2,1,0:T(1,128)}, f32[1,1,32...) fusion(f32[8,5,32768]{2,1,0:T(8,128)} %all-gather.3.cloned.1.ca, ...), kind=kLoop, calls=%fused_computation.157 | loop fusion | bytes 4980736 | tf_op jit(solution)/shard_map/slice | solution.py:34
  81.9 10.3 %fusion.80 = (f32[1,1,32768]{2,1,0:T(1,128)S(1)}, f32[1,1,32768]{2,1,0:T(1,128)S(1)}, f32[1,1,32768]{2,1,0:T(1,128)}, f32[1,1,32768]{2,1,0:T(1,128)}, f32[1,1,32...) fusion(f32[8,5,32768]{2,1,0:T(8,128)} %all-gather.3.cloned.1.ca, ...), kind=kLoop, calls=%fused_computation.156 | loop fusion | bytes 4980736 | tf_op jit(solution)/shard_map/slice | solution.py:43
  92.5 5.4 %fusion.77 = f32[17,32768]{1,0:T(8,128)S(1)} fusion(f32[17,2]{1,0:T(8,128)S(1)} %collective-permute-done.1, f32[17,32768]{1,0:T(8,128)S(1)} %broadcast_in_dim.174, f32[17,2]{1,0:T(8,128)S(1)} %collective-permute-done, f32[32768]{0:T(1024)S(1)} %bitcast.125, f32[32768]{0:T(1024)S(1)} %bitcast.126, f32[32768]{0:T(1024)S(1)} %bitcast.127, ...), kind=kLoop, calls=%fused_computation.124 | loop fusion | flops 15597568 | bytes 5177684 | tf_op jit(solution)/shard_map/mul | solution.py:43
  97.9 1.6 copy-done
  99.6 1.5 collective-permute-start.2
  101.1 3.2 %collective-permute-start.3 = (f32[17,2]{1,0:T(8,128)S(1)}, f32[17,2]{1,0:T(8,128)S(1)}, u32[]{:S(2)}, u32[]{:S(2)}) collective-permute-start(f32[17,2]{1,0:T(8,128)S(1)} %get-tuple-element.57), channel_id=1, source_target_pairs={{1,0},{2,1},{3,2},{4,3},{5,4},{6,5},{7,6},{0,7},{9,8},{10,9},{11,1... | collective-permute-start | bytes 416 | tf_op jit(solution)/shard_map/ppermute | solution.py:23
  105.1 0.9 collective-permute-done.2
  106.6 10.0 %fusion.69 = f32[17,32768]{1,0:T(8,128)S(1)} fusion(f32[17,2]{1,0:T(8,128)} %copy-done.20, f32[17,32768]{1,0:T(8,128)} %copy-done, f32[17,2]{1,0:T(8,128)S(1)} %collective-permute-done.2, f32[32768]{0:T(1024)} %bitcast.122, f32[32768]{0:T(1024)} %bitcast.123, f32[32768]{0:T(1024)} %bitcast.119, f32[17]{0:T(128)} %get-tuple-element.78, f32[32768]{0:T(1024)} %bitcast.120, ...), kind=kLoop, calls=%fused_computation.114 | loop fusion | flops 15597568 | bytes 5177684 | tf_op jit(solution)/shard_map/mul | solution.py:43
  117.6 4.5 %collective-permute-start.5 = (f32[17,2]{1,0:T(8,128)S(1)}, f32[17,2]{1,0:T(8,128)}, u32[]{:S(2)}, u32[]{:S(2)}) collective-permute-start(f32[17,2]{1,0:T(8,128)S(1)} %get-tuple-element.55), channel_id=1, source_target_pairs={{1,0},{2,1},{3,2},{4,3},{5,4},{6,5},{7,6},{0,7},{9,8},{10,9},{11,1... | collective-permute-start | bytes 416 | tf_op jit(solution)/shard_map/ppermute | solution.py:23
  122.7 1.4 eq.261
  124.1 6.4 %fusion.61 = f32[17,32768]{1,0:T(8,128)S(1)} fusion(f32[17,2]{1,0:T(8,128)} %collective-permute-done.5, f32[17,32768]{1,0:T(8,128)S(1)} %fusion.69, f32[17,2]{1,0:T(8,128)} %collective-permute-done.4, f32[32768]{0:T(1024)} %bitcast.117, f32[32768]{0:T(1024)} %bitcast.118, f32[32768]{0:T(1024)} %bitcast.114, f32[17]{0:T(128)} %get-tuple-element.79, ...), kind=kLoop, calls=%fused_computation.104 | loop fusion | flops 15597568 | bytes 5177684 | tf_op jit(solution)/shard_map/mul | solution.py:43
  130.6 1.6 copy-done.1
  133.1 3.9 %collective-permute-start.7 = (f32[17,2]{1,0:T(8,128)S(1)}, f32[17,2]{1,0:T(8,128)S(1)}, u32[]{:S(2)}, u32[]{:S(2)}) collective-permute-start(f32[17,2]{1,0:T(8,128)S(1)} %get-tuple-element.53), channel_id=1, source_target_pairs={{1,0},{2,1},{3,2},{4,3},{5,4},{6,5},{7,6},{0,7},{9,8},{10,9},{11,1... | collective-permute-start | bytes 416 | tf_op jit(solution)/shard_map/ppermute | solution.py:23
  137.0 1.7 collective-permute-done.6
  139.3 10.0 %fusion.53 = f32[17,32768]{1,0:T(8,128)S(1)} fusion(f32[17,2]{1,0:T(8,128)} %copy-done.21, f32[17,32768]{1,0:T(8,128)} %copy-done.1, f32[17,2]{1,0:T(8,128)S(1)} %collective-permute-done.6, f32[32768]{0:T(1024)} %bitcast.112, f32[32768]{0:T(1024)} %bitcast.113, f32[32768]{0:T(1024)} %bitcast.109, f32[17]{0:T(128)} %get-tuple-element.80, f32[32768]{0:T(1024)} %bitcast.110, ...), kind=kLoop, calls=%fused_computation.94 | loop fusion | flops 15597568 | bytes 5177684 | tf_op jit(solution)/shard_map/mul | solution.py:43
  150.8 3.9 %collective-permute-start.9 = (f32[17,2]{1,0:T(8,128)S(1)}, f32[17,2]{1,0:T(8,128)}, u32[]{:S(2)}, u32[]{:S(2)}) collective-permute-start(f32[17,2]{1,0:T(8,128)S(1)} %get-tuple-element.51), channel_id=1, source_target_pairs={{1,0},{2,1},{3,2},{4,3},{5,4},{6,5},{7,6},{0,7},{9,8},{10,9},{11,1... | collective-permute-start | bytes 416 | tf_op jit(solution)/shard_map/ppermute | solution.py:23
  154.7 2.0 collective-permute-done.8
  156.8 6.6 %fusion.45 = f32[17,32768]{1,0:T(8,128)S(1)} fusion(f32[17,2]{1,0:T(8,128)} %collective-permute-done.9, f32[17,32768]{1,0:T(8,128)S(1)} %fusion.53, f32[17,2]{1,0:T(8,128)} %collective-permute-done.8, f32[32768]{0:T(1024)} %bitcast.107, f32[32768]{0:T(1024)} %bitcast.108, f32[32768]{0:T(1024)} %bitcast.104, f32[17]{0:T(128)} %get-tuple-element.81, ...), kind=kLoop, calls=%fused_computation.84 | loop fusion | flops 15597568 | bytes 5177684 | tf_op jit(solution)/shard_map/mul | solution.py:43
  164.3 3.8 %collective-permute-start.11 = (f32[17,2]{1,0:T(8,128)S(1)}, f32[17,2]{1,0:T(8,128)S(1)}, u32[]{:S(2)}, u32[]{:S(2)}) collective-permute-start(f32[17,2]{1,0:T(8,128)S(1)} %get-tuple-element.49), channel_id=1, source_target_pairs={{1,0},{2,1},{3,2},{4,3},{5,4},{6,5},{7,6},{0,7},{9,8},{10,9},{11,1... | collective-permute-start | bytes 416 | tf_op jit(solution)/shard_map/ppermute | solution.py:23
  168.7 1.1 collective-permute-done.10
  169.9 5.4 %fusion.37 = f32[17,32768]{1,0:T(8,128)S(1)} fusion(f32[17,2]{1,0:T(8,128)S(1)} %collective-permute-done.11, f32[17,32768]{1,0:T(8,128)S(1)} %fusion.45, f32[17,2]{1,0:T(8,128)S(1)} %collective-permute-done.10, f32[32768]{0:T(1024)S(1)} %bitcast.102, f32[32768]{0:T(1024)S(1)} %bitcast.103, f32[32768]{0:T(1024)S(1)} %bitcast.99, f32[17]{0:T(128)S(1)} %copy-done.24, ...), kind=kLoop, calls=%fused_computation.74 | loop fusion | flops 15597568 | bytes 5177684 | tf_op jit(solution)/shard_map/mul | solution.py:43
  176.3 3.9 %collective-permute-start.13 = (f32[17,2]{1,0:T(8,128)S(1)}, f32[17,2]{1,0:T(8,128)S(1)}, u32[]{:S(2)}, u32[]{:S(2)}) collective-permute-start(f32[17,2]{1,0:T(8,128)S(1)} %get-tuple-element.47), channel_id=1, source_target_pairs={{1,0},{2,1},{3,2},{4,3},{5,4},{6,5},{7,6},{0,7},{9,8},{10,9},{11,1... | collective-permute-start | bytes 416 | tf_op jit(solution)/shard_map/ppermute | solution.py:23
  180.2 1.8 fusion.82
  182.1 5.4 %fusion.29 = f32[17,32768]{1,0:T(8,128)S(1)} fusion(f32[17,2]{1,0:T(8,128)S(1)} %collective-permute-done.13, f32[17,32768]{1,0:T(8,128)S(1)} %fusion.37, f32[17,2]{1,0:T(8,128)S(1)} %collective-permute-done.12, f32[32768]{0:T(1024)S(1)} %bitcast.97, f32[32768]{0:T(1024)S(1)} %bitcast.98, f32[32768]{0:T(1024)S(1)} %bitcast.95, f32[17]{0:T(128)S(1)} %copy-done.23, ...), kind=kLoop, calls=%fused_computation.64 | loop fusion | flops 15597568 | bytes 5177684 | tf_op jit(solution)/shard_map/mul | solution.py:43
  188.5 3.8 %collective-permute-start.15 = (f32[17,2]{1,0:T(8,128)S(1)}, f32[17,2]{1,0:T(8,128)S(1)}, u32[]{:S(2)}, u32[]{:S(2)}) collective-permute-start(f32[17,2]{1,0:T(8,128)S(1)} %get-tuple-element.45), channel_id=1, source_target_pairs={{1,0},{2,1},{3,2},{4,3},{5,4},{6,5},{7,6},{0,7},{9,8},{10,9},{11,1... | collective-permute-start | bytes 416 | tf_op jit(solution)/shard_map/ppermute | solution.py:23
  193.0 1.0 collective-permute-done.14
  194.0 5.4 %fusion.21 = f32[17,32768]{1,0:T(8,128)S(1)} fusion(f32[17,2]{1,0:T(8,128)S(1)} %collective-permute-done.15, f32[17,32768]{1,0:T(8,128)S(1)} %fusion.29, f32[17,2]{1,0:T(8,128)S(1)} %collective-permute-done.14, f32[32768]{0:T(1024)S(1)} %bitcast.93, f32[32768]{0:T(1024)S(1)} %bitcast.94, f32[32768]{0:T(1024)S(1)} %bitcast.130, f32[17]{0:T(128)S(1)} %get-tuple-element.76, ...), kind=kLoop, calls=%fused_computation.54 | loop fusion | flops 15597568 | bytes 5177684 | tf_op jit(solution)/shard_map/mul | solution.py:43
  199.6 1.8 multiply_reduce_fusion
  201.6 21.9 %all-reduce = f32[128]{0:T(128)S(1)} all-reduce(f32[128]{0:T(128)S(1)} %dynamic-update-slice), channel_id=2, replica_groups=mesh['bump'=4,'nx'=2,'ny'=4] {'nx','ny'}, use_global_device_ids=true, to_apply=%add | all-reduce | flops 128 | bytes 1024
  (134 shorter events, 21.1 us)
Async XLA Ops:
  7.2 19.2 %copy-start.28 = (f32[16]{0:T(128)S(1)}, f32[16]{0:T(128)}, u32[]{:S(2)}) copy-start(f32[16]{0:T(128)} %param.13) | copy-start | bytes 196
  7.2 19.2 %copy-start.27 = (s32[16]{0:T(128)S(1)}, s32[16]{0:T(128)}, u32[]{:S(2)}) copy-start(s32[16]{0:T(128)} %param.12) | copy-start | bytes 196
  7.2 64.7 %all-gather.3.cloned.1.call-start = ((), (), s32[]{:S(2)}) async-start(), calls=%async_computation | async-start | bytes 10485760 | tf_op jit(solution)/shard_map/all_gather | solution.py:58
  10.8 81.4 %collective-permute-start.1 = (f32[17,2]{1,0:T(8,128)S(1)}, f32[17,2]{1,0:T(8,128)S(1)}, u32[]{:S(2)}, u32[]{:S(2)}) collective-permute-start(f32[17,2]{1,0:T(8,128)S(1)} %broadcast_in_dim.178), channel_id=1, source_target_pairs={{1,0},{2,1},{3,2},{4,3},{5,4},{6,5},{7,6},{0,7},{9,8},{10,9},{11,1... | collective-permute-start | bytes 416 | tf_op jit(solution)/shard_map/ppermute | solution.py:23
  16.9 75.4 %collective-permute-start = (f32[17,2]{1,0:T(8,128)S(1)}, f32[17,2]{1,0:T(8,128)S(1)}, u32[]{:S(2)}, u32[]{:S(2)}) collective-permute-start(f32[17,2]{1,0:T(8,128)S(1)} %broadcast_in_dim.175), channel_id=1, source_target_pairs={{0,1},{1,2},{2,3},{3,4},{4,5},{5,6},{6,7},{7,0},{8,9},{9,10},{10,1... | collective-permute-start | bytes 416 | tf_op jit(solution)/shard_map/ppermute | solution.py:22
  99.6 6.4 %collective-permute-start.2 = (f32[17,2]{1,0:T(8,128)S(1)}, f32[17,2]{1,0:T(8,128)S(1)}, u32[]{:S(2)}, u32[]{:S(2)}) collective-permute-start(f32[17,2]{1,0:T(8,128)S(1)} %get-tuple-element.56), channel_id=1, source_target_pairs={{0,1},{1,2},{2,3},{3,4},{4,5},{5,6},{6,7},{7,0},{8,9},{9,10},{10,1... | collective-permute-start | bytes 416 | tf_op jit(solution)/shard_map/ppermute | solution.py:22
  101.1 4.9 %collective-permute-start.3 = (f32[17,2]{1,0:T(8,128)S(1)}, f32[17,2]{1,0:T(8,128)S(1)}, u32[]{:S(2)}, u32[]{:S(2)}) collective-permute-start(f32[17,2]{1,0:T(8,128)S(1)} %get-tuple-element.57), channel_id=1, source_target_pairs={{1,0},{2,1},{3,2},{4,3},{5,4},{6,5},{7,6},{0,7},{9,8},{10,9},{11,1... | collective-permute-start | bytes 416 | tf_op jit(solution)/shard_map/ppermute | solution.py:23
  106.6 15.4 %copy-start.25 = (pred[128]{0:T(512)(128)(4,1)S(1)}, pred[128]{0:T(512)(128)(4,1)}, u32[]{:S(2)}) copy-start(pred[128]{0:T(512)(128)(4,1)} %get-tuple-element.73) | copy-start | bytes 388
  117.3 6.8 %collective-permute-start.4 = (f32[17,2]{1,0:T(8,128)}, f32[17,2]{1,0:T(8,128)}, u32[]{:S(2)}, u32[]{:S(2)}) collective-permute-start(f32[17,2]{1,0:T(8,128)} %get-tuple-element.54), channel_id=1, source_target_pairs={{0,1},{1,2},{2,3},{3,4},{4,5},{5,6},{6,7},{7,0},{8,9},{9,10},{10,1... | collective-permute-start | bytes 416 | tf_op jit(solution)/shard_map/ppermute | solution.py:22
  117.6 6.5 %collective-permute-start.5 = (f32[17,2]{1,0:T(8,128)S(1)}, f32[17,2]{1,0:T(8,128)}, u32[]{:S(2)}, u32[]{:S(2)}) collective-permute-start(f32[17,2]{1,0:T(8,128)S(1)} %get-tuple-element.55), channel_id=1, source_target_pairs={{1,0},{2,1},{3,2},{4,3},{5,4},{6,5},{7,6},{0,7},{9,8},{10,9},{11,1... | collective-permute-start | bytes 416 | tf_op jit(solution)/shard_map/ppermute | solution.py:23
  132.3 6.4 %collective-permute-start.6 = (f32[17,2]{1,0:T(8,128)S(1)}, f32[17,2]{1,0:T(8,128)S(1)}, u32[]{:S(2)}, u32[]{:S(2)}) collective-permute-start(f32[17,2]{1,0:T(8,128)S(1)} %get-tuple-element.52), channel_id=1, source_target_pairs={{0,1},{1,2},{2,3},{3,4},{4,5},{5,6},{6,7},{7,0},{8,9},{9,10},{10,1... | collective-permute-start | bytes 416 | tf_op jit(solution)/shard_map/ppermute | solution.py:22
  133.1 5.6 %collective-permute-start.7 = (f32[17,2]{1,0:T(8,128)S(1)}, f32[17,2]{1,0:T(8,128)S(1)}, u32[]{:S(2)}, u32[]{:S(2)}) collective-permute-start(f32[17,2]{1,0:T(8,128)S(1)} %get-tuple-element.53), channel_id=1, source_target_pairs={{1,0},{2,1},{3,2},{4,3},{5,4},{6,5},{7,6},{0,7},{9,8},{10,9},{11,1... | collective-permute-start | bytes 416 | tf_op jit(solution)/shard_map/ppermute | solution.py:23
  150.0 6.7 %collective-permute-start.8 = (f32[17,2]{1,0:T(8,128)}, f32[17,2]{1,0:T(8,128)}, u32[]{:S(2)}, u32[]{:S(2)}) collective-permute-start(f32[17,2]{1,0:T(8,128)} %get-tuple-element.50), channel_id=1, source_target_pairs={{0,1},{1,2},{2,3},{3,4},{4,5},{5,6},{6,7},{7,0},{8,9},{9,10},{10,1... | collective-permute-start | bytes 416 | tf_op jit(solution)/shard_map/ppermute | solution.py:22
  150.8 5.9 %collective-permute-start.9 = (f32[17,2]{1,0:T(8,128)S(1)}, f32[17,2]{1,0:T(8,128)}, u32[]{:S(2)}, u32[]{:S(2)}) collective-permute-start(f32[17,2]{1,0:T(8,128)S(1)} %get-tuple-element.51), channel_id=1, source_target_pairs={{1,0},{2,1},{3,2},{4,3},{5,4},{6,5},{7,6},{0,7},{9,8},{10,9},{11,1... | collective-permute-start | bytes 416 | tf_op jit(solution)/shard_map/ppermute | solution.py:23
  156.7 13.1 %copy-start.7 = (f32[1,1,32768]{2,1,0:T(1,128)S(1)}, f32[1,1,32768]{2,1,0:T(1,128)}, u32[]{:S(2)}) copy-start(f32[1,1,32768]{2,1,0:T(1,128)} %get-tuple-element.37) | copy-start | bytes 393220
  156.7 13.1 %copy-start.8 = (f32[1,1,32768]{2,1,0:T(1,128)S(1)}, f32[1,1,32768]{2,1,0:T(1,128)}, u32[]{:S(2)}) copy-start(f32[1,1,32768]{2,1,0:T(1,128)} %get-tuple-element.38) | copy-start | bytes 393220
  156.7 13.1 %copy-start.9 = (f32[1,1,32768]{2,1,0:T(1,128)S(1)}, f32[1,1,32768]{2,1,0:T(1,128)}, u32[]{:S(2)}) copy-start(f32[1,1,32768]{2,1,0:T(1,128)} %get-tuple-element.39) | copy-start | bytes 393220
  156.7 13.1 %copy-start.10 = (f32[1,1,32768]{2,1,0:T(1,128)S(1)}, f32[1,1,32768]{2,1,0:T(1,128)}, u32[]{:S(2)}) copy-start(f32[1,1,32768]{2,1,0:T(1,128)} %get-tuple-element.9) | copy-start | bytes 393220
  156.7 13.1 %copy-start.11 = (f32[1,1,32768]{2,1,0:T(1,128)S(1)}, f32[1,1,32768]{2,1,0:T(1,128)}, u32[]{:S(2)}) copy-start(f32[1,1,32768]{2,1,0:T(1,128)} %get-tuple-element.10) | copy-start | bytes 393220
  156.7 13.1 %copy-start.16 = (pred[32768]{0:T(1024)(128)(4,1)S(1)}, pred[32768]{0:T(1024)(128)(4,1)}, u32[]{:S(2)}) copy-start(pred[32768]{0:T(1024)(128)(4,1)} %eq.297) | copy-start | bytes 98308
  156.7 13.1 %copy-start.17 = (pred[32768]{0:T(1024)(128)(4,1)S(1)}, pred[32768]{0:T(1024)(128)(4,1)}, u32[]{:S(2)}) copy-start(pred[32768]{0:T(1024)(128)(4,1)} %eq.264) | copy-start | bytes 98308
  156.8 13.1 %copy-start.24 = (f32[17]{0:T(128)S(1)}, f32[17]{0:T(128)}, u32[]{:S(2)}) copy-start(f32[17]{0:T(128)} %get-tuple-element.82) | copy-start | bytes 208
  163.4 6.4 %collective-permute-start.10 = (f32[17,2]{1,0:T(8,128)S(1)}, f32[17,2]{1,0:T(8,128)S(1)}, u32[]{:S(2)}, u32[]{:S(2)}) collective-permute-start(f32[17,2]{1,0:T(8,128)S(1)} %get-tuple-element.48), channel_id=1, source_target_pairs={{0,1},{1,2},{2,3},{3,4},{4,5},{5,6},{6,7},{7,0},{8,9},{9,10},{10,1... | collective-permute-start | bytes 416 | tf_op jit(solution)/shard_map/ppermute | solution.py:22
  164.3 5.5 %collective-permute-start.11 = (f32[17,2]{1,0:T(8,128)S(1)}, f32[17,2]{1,0:T(8,128)S(1)}, u32[]{:S(2)}, u32[]{:S(2)}) collective-permute-start(f32[17,2]{1,0:T(8,128)S(1)} %get-tuple-element.49), channel_id=1, source_target_pairs={{1,0},{2,1},{3,2},{4,3},{5,4},{6,5},{7,6},{0,7},{9,8},{10,9},{11,1... | collective-permute-start | bytes 416 | tf_op jit(solution)/shard_map/ppermute | solution.py:23
  169.9 12.1 %copy-start.3 = (f32[1,1,32768]{2,1,0:T(1,128)S(1)}, f32[1,1,32768]{2,1,0:T(1,128)}, u32[]{:S(2)}) copy-start(f32[1,1,32768]{2,1,0:T(1,128)} %get-tuple-element.40) | copy-start | bytes 393220
  169.9 12.1 %copy-start.4 = (f32[1,1,32768]{2,1,0:T(1,128)S(1)}, f32[1,1,32768]{2,1,0:T(1,128)}, u32[]{:S(2)}) copy-start(f32[1,1,32768]{2,1,0:T(1,128)} %get-tuple-element.41) | copy-start | bytes 393220
  169.9 12.1 %copy-start.5 = (f32[1,1,32768]{2,1,0:T(1,128)S(1)}, f32[1,1,32768]{2,1,0:T(1,128)}, u32[]{:S(2)}) copy-start(f32[1,1,32768]{2,1,0:T(1,128)} %get-tuple-element.7) | copy-start | bytes 393220
  175.4 6.5 %collective-permute-start.12 = (f32[17,2]{1,0:T(8,128)S(1)}, f32[17,2]{1,0:T(8,128)S(1)}, u32[]{:S(2)}, u32[]{:S(2)}) collective-permute-start(f32[17,2]{1,0:T(8,128)S(1)} %get-tuple-element.46), channel_id=1, source_target_pairs={{0,1},{1,2},{2,3},{3,4},{4,5},{5,6},{6,7},{7,0},{8,9},{9,10},{10,1... | collective-permute-start | bytes 416 | tf_op jit(solution)/shard_map/ppermute | solution.py:22
  176.3 5.7 %collective-permute-start.13 = (f32[17,2]{1,0:T(8,128)S(1)}, f32[17,2]{1,0:T(8,128)S(1)}, u32[]{:S(2)}, u32[]{:S(2)}) collective-permute-start(f32[17,2]{1,0:T(8,128)S(1)} %get-tuple-element.47), channel_id=1, source_target_pairs={{1,0},{2,1},{3,2},{4,3},{5,4},{6,5},{7,6},{0,7},{9,8},{10,9},{11,1... | collective-permute-start | bytes 416 | tf_op jit(solution)/shard_map/ppermute | solution.py:23
  187.6 6.4 %collective-permute-start.14 = (f32[17,2]{1,0:T(8,128)S(1)}, f32[17,2]{1,0:T(8,128)S(1)}, u32[]{:S(2)}, u32[]{:S(2)}) collective-permute-start(f32[17,2]{1,0:T(8,128)S(1)} %get-tuple-element.44), channel_id=1, source_target_pairs={{0,1},{1,2},{2,3},{3,4},{4,5},{5,6},{6,7},{7,0},{8,9},{9,10},{10,1... | collective-permute-start | bytes 416 | tf_op jit(solution)/shard_map/ppermute | solution.py:22
  188.5 5.5 %collective-permute-start.15 = (f32[17,2]{1,0:T(8,128)S(1)}, f32[17,2]{1,0:T(8,128)S(1)}, u32[]{:S(2)}, u32[]{:S(2)}) collective-permute-start(f32[17,2]{1,0:T(8,128)S(1)} %get-tuple-element.45), channel_id=1, source_target_pairs={{1,0},{2,1},{3,2},{4,3},{5,4},{6,5},{7,6},{0,7},{9,8},{10,9},{11,1... | collective-permute-start | bytes 416 | tf_op jit(solution)/shard_map/ppermute | solution.py:23
  199.5 24.2 %copy-start.29 = (f32[16]{0:T(128)S(1)}, f32[16]{0:T(128)}, u32[]{:S(2)}) copy-start(f32[16]{0:T(128)} %param.13) | copy-start | bytes 196
  (16 other events, 128.8 us)
Sparse Core Ops, SparseCore 0:
  10.9 60.9 all-gather.2
